TPU v7x, 32 devices: a whole 2x2x4 slice. The times are simulated.
32 devices in a mesh: grp: 4 (over x, core), shard: 8 (over z, y).
Axes of the slice: x: 2, y: 2, z: 4, core: 2. Of those that a mesh axis runs over, the one named last changes fastest.
Arguments:
- inputs: bfloat16 [16384, 1024], P(('grp', 'shard')), may hold values from -6 to 6
- cotangent: bfloat16 [16384, 1024], P(('grp', 'shard')), may hold values from -6 to 6
- doc_ids: int32 [16384], P(('grp', 'shard')), may hold values from 0 to 1, as said below
- master_in: float32 [1024, 7168], P('shard'), may hold values from -0.1875 to 0.1875
- master_out: float32 [5120, 1024], P('shard'), may hold values from -6 to 6
- vectors: float32 [12, 1024], P(None, 'shard'), may hold values from -2 to 2, as said below
- moment_in: float32 [1024, 7168], P('shard'), may hold values from -24 to 24
- moment_out: float32 [5120, 1024], P('shard'), may hold values from -24 to 24
- moment_vec: float32 [12, 1024], P(None, 'shard'), may hold values from -24 to 24
- square_in: float32 [1024, 7168], P('shard'), may hold values from 4 to 1000
- square_out: float32 [5120, 1024], P('shard'), may hold values from 4 to 1000
- square_vec: float32 [12, 1024], P(None, 'shard'), may hold values from 4 to 1000
Outputs:
- output: bfloat16 [16384, 1024], P(('grp', 'shard'))
- input_grad: float32 [16384, 1024], P(('grp', 'shard'))
- grad_in: float32 [1024, 7168], P('shard')
- grad_out: float32 [5120, 1024], P('shard')
- grad_vec: float32 [12, 1024], P(None, 'shard')
- update_in: float32 [1024, 7168], P('shard')
- update_out: float32 [5120, 1024], P('shard')
- update_vec: float32 [12, 1024], P(None, 'shard')
- moment_in_next: float32 [1024, 7168], P('shard')
- moment_out_next: float32 [5120, 1024], P('shard')
- moment_vec_next: float32 [12, 1024], P(None, 'shard')
- square_in_next: float32 [1024, 7168], P('shard')
- square_out_next: float32 [5120, 1024], P('shard')
- square_vec_next: float32 [12, 1024], P(None, 'shard')
Inputs may be any that keep to these rules, and one draw needn't show every extreme that they name: `doc_ids`: on each device the ids never fall along its 512 slots; each id j < 1 covers 8 to 512 slots in a row; id 1 covers the padding after them; on some device every sequence has 512 slots. `vectors`: rows 0 and 2 lie between 0.6 and 1.4.
All inputs are finite; a program needn't handle non-finite values.
Results may differ from a plain program's by a relative error of at most 0.035.
Values may be sent and summed in bfloat16 or wider, within the bound.
A program may use at most 320 MiB of HBM per device.

v0:
```python
import jax
import jax.numpy as jnp
from jax import lax
from jax.sharding import PartitionSpec as P

HEAD = 64
ROT = 16
SEQ_DEV = 1
STEP = 10
NEG = -1e30


def rotary_tables(doc_ids):
    count = doc_ids.shape[0]
    order = jnp.arange(count, dtype=jnp.int32)
    first = jnp.sum((doc_ids[None, :] < doc_ids[:, None]).astype(jnp.int32), axis=1)
    position = (order - first).astype(jnp.float32)
    half = ROT // 2
    freq = 10000.0 ** (-(jnp.arange(half, dtype=jnp.float32) * 2.0 / ROT))
    angle = position[:, None] * freq[None, :]
    angle = jnp.concatenate([angle, angle], axis=1)
    return (jnp.cos(angle), jnp.sin(angle))


def rotate(values, cosine, sine):
    half = ROT // 2
    part = values[..., :ROT]
    turned = jnp.concatenate([-part[..., half:], part[..., :half]], axis=-1)
    moved = part * cosine[:, None, :] + turned * sine[:, None, :]
    return jnp.concatenate([moved, values[..., ROT:]], axis=-1)


def rotate_back(grads, cosine, sine):
    half = ROT // 2
    part = grads[..., :ROT]
    scaled = part * sine[:, None, :]
    turned = jnp.concatenate([scaled[..., half:], -scaled[..., :half]], axis=-1)
    moved = part * cosine[:, None, :] + turned
    return jnp.concatenate([moved, grads[..., ROT:]], axis=-1)


def layer_norm_apply(residual_stream, norm_gain, norm_offset):
    feature_mean = jnp.mean(residual_stream, axis=-1, keepdims=True)
    mean_removed = residual_stream - feature_mean
    var = jnp.mean(mean_removed * mean_removed, axis=-1, keepdims=True)
    inverse_deviation = lax.rsqrt(var + 1e-05)
    normalized_input = mean_removed * inverse_deviation
    return (normalized_input * norm_gain + norm_offset, normalized_input, inverse_deviation)


def layer_norm_gradient(gradient_norm_output, normalized_input, inverse_deviation, norm_gain):
    gradient_normalized = gradient_norm_output * norm_gain
    gradient_stream = inverse_deviation * (
        gradient_normalized
        - jnp.mean(gradient_normalized, axis=-1, keepdims=True)
        - normalized_input
        * jnp.mean(gradient_normalized * normalized_input, axis=-1, keepdims=True)
    )
    return (
        gradient_stream,
        jnp.sum(gradient_norm_output * normalized_input, axis=0),
        jnp.sum(gradient_norm_output, axis=0),
    )


def unpack(packed, width):
    vec = packed.astype(jnp.float32)
    return (
        vec[0],
        vec[1],
        vec[2],
        vec[3],
        vec[4:7].reshape(3 * width),
        vec[7:11].reshape(4 * width),
        vec[11],
    )


def mask_block(doc_ids, start, stop):
    rows = jnp.arange(start, stop)[:, None]
    cols = jnp.arange(stop)[None, :]
    return (doc_ids[start:stop, None] == doc_ids[None, :stop]) & (cols <= rows)


def block_scores(query, keys, allowed, scale):
    raw = jnp.einsum("qhd,khd->hqk", query, keys, preferred_element_type=jnp.float32) * scale
    return jnp.where(allowed[None], raw, NEG)


def gelu_value(hidden):
    return 0.5 * hidden * (1.0 + lax.erf(hidden * 0.7071067811865476))


def gelu_slope(hidden):
    return (
        0.5 * (1.0 + lax.erf(hidden * 0.7071067811865476))
        + hidden * jnp.exp(-0.5 * hidden * hidden) * 0.3989422804014327
    )


def contract_rows(left, right):
    return lax.dot_general(
        left, right, (((0,), (0,)), ((), ())), preferred_element_type=jnp.float32
    )


def contract_cols(left, right):
    return lax.dot_general(
        left, right, (((1,), (1,)), ((), ())), preferred_element_type=jnp.float32
    )


def adam(master, moment, square, grad, decay):
    moment_next = 0.9 * moment + 0.1 * grad
    square_next = 0.95 * square + 0.05 * grad * grad
    ratio = moment_next / (1.0 - 0.9**STEP) / (jnp.sqrt(square_next / (1.0 - 0.95**STEP)) + 1e-08)
    return (-0.03 * (ratio + decay * master), moment_next, square_next)


def shards(
    inputs,
    cotangent,
    doc_ids,
    master_in,
    master_out,
    vectors,
    moment_in,
    moment_out,
    moment_vec,
    square_in,
    square_out,
    square_vec,
):
    slots, width = inputs.shape
    heads = width // HEAD
    block = min(512, slots)
    scale = HEAD ** (-0.5)
    live = (doc_ids < SEQ_DEV).astype(jnp.float32)[:, None]
    cosine, sine = rotary_tables(doc_ids)
    w_in, w_out, packed = (
        lax.all_gather(master_in.astype(jnp.bfloat16), "shard", axis=0, tiled=True),
        lax.all_gather(master_out.astype(jnp.bfloat16), "shard", axis=0, tiled=True),
        lax.all_gather(vectors.astype(jnp.bfloat16), "shard", axis=1, tiled=True),
    )
    (
        first_norm_gain,
        first_norm_offset,
        second_norm_gain,
        second_norm_offset,
        bias_qkv,
        bias_hidden,
        bias_out,
    ) = unpack(packed, width)
    residual_stream = inputs.astype(jnp.float32)
    branch_input_first, first_normalized, first_inverse_deviation = layer_norm_apply(
        residual_stream, first_norm_gain, first_norm_offset
    )
    branch_input_second, second_normalized, second_inverse_deviation = layer_norm_apply(
        residual_stream, second_norm_gain, second_norm_offset
    )
    branch_input_first = branch_input_first.astype(jnp.bfloat16)
    branch_input_second = branch_input_second.astype(jnp.bfloat16)
    qkv = (
        jnp.dot(branch_input_first, w_in[:, : 3 * width], preferred_element_type=jnp.float32)
        + bias_qkv
    )
    hidden = (
        jnp.dot(branch_input_second, w_in[:, 3 * width :], preferred_element_type=jnp.float32)
        + bias_hidden
    )
    query = rotate(qkv[:, :width].reshape(slots, heads, HEAD), cosine, sine).astype(jnp.bfloat16)
    keys = rotate(qkv[:, width : 2 * width].reshape(slots, heads, HEAD), cosine, sine).astype(
        jnp.bfloat16
    )
    values = qkv[:, 2 * width :].reshape(slots, heads, HEAD).astype(jnp.bfloat16)
    start = 0
    stop = start + block
    allowed = mask_block(doc_ids, start, stop)
    scores = block_scores(query, keys, allowed, scale)
    top = jnp.max(scores, axis=-1, keepdims=True)
    expo = jnp.exp(scores - top)
    total = jnp.sum(expo, axis=-1, keepdims=True)
    probs = (expo / total).astype(jnp.bfloat16)
    totals = [top + jnp.log(total)]
    attended_parts = jnp.einsum("hqk,khd->qhd", probs, values, preferred_element_type=jnp.float32)
    attended = attended_parts.reshape(slots, width).astype(jnp.bfloat16)
    active = gelu_value(hidden).astype(jnp.bfloat16)
    joined = jnp.concatenate([attended, active], axis=1)
    branch = jnp.dot(joined, w_out, preferred_element_type=jnp.float32) + bias_out
    output = ((residual_stream + branch) * live).astype(jnp.bfloat16)
    d_out = cotangent.astype(jnp.float32) * live
    d_out_low = d_out.astype(jnp.bfloat16)
    d_joined = contract_cols(d_out_low, w_out)
    grad_out_term = contract_rows(joined, d_out_low)
    d_attended = d_joined[:, :width].reshape(slots, heads, HEAD).astype(jnp.bfloat16)
    d_hidden = (d_joined[:, width:] * gelu_slope(hidden)).astype(jnp.bfloat16)
    d_query_parts = []
    d_keys = jnp.zeros((slots, heads, HEAD), jnp.float32)
    d_values = jnp.zeros((slots, heads, HEAD), jnp.float32)
    for number, start in enumerate(range(0, slots, block)):
        stop = start + block
        allowed = mask_block(doc_ids, start, stop)
        scores = block_scores(query, keys, allowed, scale)
        probs = jnp.exp(scores - totals[number])
        d_probs = jnp.einsum("qhd,khd->hqk", d_attended, values, preferred_element_type=jnp.float32)
        weighted = jnp.sum(probs * d_probs, axis=-1, keepdims=True)
        d_scores = (probs * (d_probs - weighted)).astype(jnp.bfloat16)
        d_query_parts.append(
            jnp.einsum("hqk,khd->qhd", d_scores, keys, preferred_element_type=jnp.float32) * scale
        )
        d_keys = d_keys.at[:stop].add(
            jnp.einsum("hqk,qhd->khd", d_scores, query, preferred_element_type=jnp.float32) * scale
        )
        d_values = d_values.at[:stop].add(
            jnp.einsum(
                "hqk,qhd->khd",
                probs.astype(jnp.bfloat16),
                d_attended,
                preferred_element_type=jnp.float32,
            )
        )
    d_query = rotate_back(d_query_parts[0], cosine, sine)
    d_keys = rotate_back(d_keys, cosine, sine)
    d_qkv = jnp.concatenate(
        [
            d_query.reshape(slots, width),
            d_keys.reshape(slots, width),
            d_values.reshape(slots, width),
        ],
        axis=1,
    ).astype(jnp.bfloat16)
    grad_in_term = jnp.concatenate(
        [contract_rows(branch_input_first, d_qkv), contract_rows(branch_input_second, d_hidden)],
        axis=1,
    )
    gradient_branch_first = contract_cols(d_qkv, w_in[:, : 3 * width])
    gradient_branch_second = contract_cols(d_hidden, w_in[:, 3 * width :])
    gradient_stream_first, gradient_gain_first, gradient_offset_first = layer_norm_gradient(
        gradient_branch_first, first_normalized, first_inverse_deviation, first_norm_gain
    )
    gradient_stream_second, gradient_gain_second, gradient_offset_second = layer_norm_gradient(
        gradient_branch_second, second_normalized, second_inverse_deviation, second_norm_gain
    )
    input_grad = d_out + gradient_stream_first + gradient_stream_second
    grad_vec_term = jnp.concatenate(
        [
            gradient_gain_first[None],
            gradient_offset_first[None],
            gradient_gain_second[None],
            gradient_offset_second[None],
            jnp.sum(d_qkv, axis=0, dtype=jnp.float32).reshape(3, width),
            jnp.sum(d_hidden, axis=0, dtype=jnp.float32).reshape(4, width),
            jnp.sum(d_out, axis=0)[None],
        ],
        axis=0,
    )
    part_in, part_out, part_vec = (
        lax.psum_scatter(
            grad_in_term.astype(jnp.bfloat16), "shard", scatter_dimension=0, tiled=True
        ).astype(jnp.float32),
        lax.psum_scatter(
            grad_out_term.astype(jnp.bfloat16), "shard", scatter_dimension=0, tiled=True
        ).astype(jnp.float32),
        lax.psum_scatter(
            grad_vec_term.astype(jnp.bfloat16), "shard", scatter_dimension=1, tiled=True
        ).astype(jnp.float32),
    )
    grad_in, grad_out, grad_vec = (
        lax.psum(part_in.astype(jnp.bfloat16), "grp").astype(jnp.float32),
        lax.psum(part_out.astype(jnp.bfloat16), "grp").astype(jnp.float32),
        lax.psum(part_vec.astype(jnp.bfloat16), "grp").astype(jnp.float32),
    )
    update_in, moment_in_next, square_in_next = adam(master_in, moment_in, square_in, grad_in, 0.1)
    update_out, moment_out_next, square_out_next = adam(
        master_out, moment_out, square_out, grad_out, 0.1
    )
    update_vec, moment_vec_next, square_vec_next = adam(
        vectors, moment_vec, square_vec, grad_vec, 0.0
    )
    return (
        output,
        input_grad,
        grad_in,
        grad_out,
        grad_vec,
        update_in,
        update_out,
        update_vec,
        moment_in_next,
        moment_out_next,
        moment_vec_next,
        square_in_next,
        square_out_next,
        square_vec_next,
    )


def solution(mesh):
    placed = (
        P(("grp", "shard"), None),
        P(("grp", "shard"), None),
        P(("grp", "shard")),
        P("shard", None),
        P("shard", None),
        P(None, "shard"),
        P("shard", None),
        P("shard", None),
        P(None, "shard"),
        P("shard", None),
        P("shard", None),
        P(None, "shard"),
    )
    return jax.shard_map(
        shards,
        mesh=mesh,
        in_specs=placed,
        out_specs=(
            P(("grp", "shard"), None),
            P(("grp", "shard"), None),
            P("shard", None),
            P("shard", None),
            P(None, "shard"),
            P("shard", None),
            P("shard", None),
            P(None, "shard"),
            P("shard", None),
            P("shard", None),
            P(None, "shard"),
            P("shard", None),
            P("shard", None),
            P(None, "shard"),
        ),
        check_vma=False,
    )
```

profile of v0, /device:TPU:0, one launch (start us, length us, event | category | flops | bytes accessed | tf_op | source)
XLA Modules:
  0.0 945.5 jit_solution(10048721570027155907)
XLA Ops:
  12.3 28.7 %all_gather.9 = bf16[12,1024]{1,0:T(8,128)(2,1)S(1)} all-gather(bf16[12,128]{1,0:T(8,128)(2,1)S(1)} %convert_element_type.105), channel_id=1, replica_groups=mesh['grp'=4,'shard'=8] {'shard'}, dimensions={1}, use_global_device_ids=true | all-gather | bytes 27648 | tf_op jit(solution)/shard_map/all_gather | solution.py:143
  45.5 170.2 %all-gather.3.cloned.1.call-done = bf16[1024,7168]{1,0:T(8,128)(2,1)} async-done(((bf16[128,7168]{1,0:T(8,128)(2,1)}), bf16[1024,7168]{1,0:T(8,128)(2,1)}) %all-gather.3.cloned.1.call-update) | async-done | bytes 14680080 | tf_op jit(solution)/shard_map/all_gather | solution.py:141
  215.7 5.8 fusion.20
  225.6 4.4 fusion.87
  241.9 7.3 fusion.91
  249.3 8.4 fusion
  257.8 7.6 fusion.55
  266.0 10.3 %multiply_convert_fusion.1 = (bf16[512,4096]{1,0:T(8,128)(2,1)S(1)}, f32[512,4096]{1,0:T(8,128)}) fusion(f32[4096]{0:T(1024)S(1)} %bitcast.61, bf16[1024,7168]{1,0:T(8,128)(2,1)} %all-gather.3.cloned.1.call-done, bf16[512,1024]{1,0:T(8,128)(2,1)S(1)} %copy-done.2, f32[1024]{0:T(1024)S(1)} %bitcast.73, f32[1024]{0:T(1024)S(1)} %bitcast.68, ...), kind=kOutput, calls=%fused_computation.19 | convolution fusion | flops 4310695936 | bytes 22048768 | tf_op jit(solution)/shard_map/dot_general | solution.py:168
  278.7 8.9 convolution_convert_fusion
  287.6 79.6 %all-gather.5.cloned.1.call-done = bf16[5120,1024]{1,0:T(8,128)(2,1)} async-done(((bf16[640,1024]{1,0:T(8,128)(2,1)}), bf16[5120,1024]{1,0:T(8,128)(2,1)}) %all-gather.5.cloned.1.call-update) | async-done | bytes 10485776 | tf_op jit(solution)/shard_map/all_gather | solution.py:142
  367.2 8.4 fusion.67
  375.7 4.0 copy-done.4
  381.1 14.4 %multiply_reduce_fusion = (f32[16,512]{1,0:T(8,128)}, f32[16,512,512]{1,2,0:T(8,128)}) fusion(f32[16,512,512]{1,2,0:T(8,128)} %get-tuple-element.110, f32[16,512]{1,0:T(8,128)} %log_add_fusion, bf16[512,16,64]{0,2,1:T(8,128)(2,1)S(1)} %bitcast.40, bf16[512,16,64]{0,2,1:T(8,128)(2,1)} %bitcast.48), kind=kOutput, calls=%fused_computation.1 | convolution fusion | flops 549445632 | bytes 35717120 | tf_op jit(solution)/shard_map/qhd,khd->hqk/dot_general | solution.py:205
  398.0 10.8 %multiply_convert_fusion = bf16[16,512,512]{1,2,0:T(8,128)(2,1)} fusion(f32[16,512,512]{1,2,0:T(8,128)} %get-tuple-element.112, f32[16,512,512]{1,2,0:T(8,128)S(1)} %bitcast.39, f32[16,512]{1,0:T(8,128)} %get-tuple-element.111, f32[16,512]{1,0:T(8,128)} %log_add_fusion), kind=kLoop, calls=%fused_computation | loop fusion | flops 16777216 | bytes 42008576 | tf_op jit(solution)/shard_map/convert_element_type | solution.py:207
  408.8 6.1 multiply_bitcast_fusion
  415.1 5.1 multiply_bitcast_fusion.1
  423.3 4.6 fusion.56
  427.9 6.0 convolution_convert_fusion.2
  433.9 8.1 fusion.85
  442.1 5.3 convolution_convert_fusion.1
  447.4 10.6 %pad_maximum_fusion = bf16[1024,7168]{1,0:T(8,128)(2,1)} fusion(bf16[1024,4096]{1,0:T(8,128)(2,1)S(1)} %convolution_convert_fusion.1, bf16[1024,3072]{1,0:T(8,128)(2,1)S(1)} %convolution_convert_fusion.2), kind=kLoop, calls=%fused_computation.7 | loop fusion | flops 29360128 | bytes 29360128 | tf_op jit(solution)/shard_map/concatenate | solution.py:232
  458.2 9.0 fusion.12
  467.3 9.4 fusion.48
  477.8 4.2 fusion.53
  483.1 64.1 %reduce-scatter.8.cloned.1.call-done = bf16[640,1024]{1,0:T(8,128)(2,1)} async-done(((bf16[5120,1024]{1,0:T(8,128)(2,1)}), bf16[640,1024]{1,0:T(8,128)(2,1)}) %reduce-scatter.8.cloned.1.call-update) | async-done | bytes 1310736 | tf_op jit(solution)/shard_map/reduce_scatter | solution.py:261
  547.2 239.2 %reduce-scatter.6.cloned.1.call-done = bf16[128,7168]{1,0:T(8,128)(2,1)} async-done(((bf16[1024,7168]{1,0:T(8,128)(2,1)}), bf16[128,7168]{1,0:T(8,128)(2,1)}) %reduce-scatter.6.cloned.1.call-update) | async-done | bytes 1835024 | tf_op jit(solution)/shard_map/reduce_scatter | solution.py:258
  786.5 11.2 %fusion.52 = bf16[512,1024]{1,0:T(8,128)(2,1)} fusion(bf16[512,1024]{1,0:T(8,128)(2,1)S(1)} %copy-done.3, bf16[5120,1024]{1,0:T(8,128)(2,1)} %all-gather.5.cloned.1.call-done, bf16[512,4096]{1,0:T(8,128)(2,1)} %copy-done.49, bf16[512,1024]{1,0:T(8,128)(2,1)S(1)} %copy-done.23, f32[512]{0:T(512)S(1)} %copy-done.40, f32[1024]{0:T(1024)S(1)} %bitcast.72), kind=kOutput, calls=%fused_computation.73 | convolution fusion | flops 5381816320 | bytes 17831936 | tf_op jit(solution)/shard_map/dot_general | solution.py:189
  797.8 53.7 %reduce-scatter.10.cloned.1.call-done = bf16[128,12]{1,0:T(8,128)(2,1)} async-done(((bf16[1024,12]{1,0:T(8,128)(2,1)}), bf16[128,12]{1,0:T(8,128)(2,1)}) %reduce-scatter.10.cloned.1.call-update) | async-done | bytes 3088
  852.2 5.7 psum.23
  858.6 62.7 %all-reduce.3.cloned.1.call-done = (bf16[128,7168]{1,0:T(8,128)(2,1)}, bf16[640,1024]{1,0:T(8,128)(2,1)}) async-done(((bf16[128,7168]{1,0:T(8,128)(2,1)}, bf16[640,1024]{1,0:T(8,128)(2,1)}), (bf16[128,7168]{1,0:T(8,128)(2,1)}, bf16[640,1024]{1,0:T(8,128)(2,1)})) %all-reduce.3.cloned.1.call-update) | async-done | bytes 3145744 | tf_op jit(solution)/shard_map/psum | solution.py:269
  921.3 10.9 %add_multiply_fusion = (f32[128,7168]{1,0:T(8,128)}, f32[128,7168]{1,0:T(8,128)}, f32[128,7168]{1,0:T(8,128)}, f32[128,7168]{1,0:T(8,128)}) fusion(f32[128,7168]{1,0:T(8,128)} %param.23, f32[128,7168]{1,0:T(8,128)} %param.26, f32[128,7168]{1,0:T(8,128)} %param.29, bf16[128,7168]{1,0:T(8,128)(2,1)} %get-tuple-element.66), kind=kLoop, calls=%fused_computation.37 | loop fusion | flops 13762560 | bytes 27525120 | tf_op jit(solution)/shard_map/mul | solution.py:117
  933.7 4.7 add_multiply_fusion.1
  (176 shorter events, 40.7 us)
Async XLA Ops:
  7.2 208.5 %all-gather.3.cloned.1.call-start = ((), (), s32[]{:S(2)}) async-start(), calls=%async_computation.3 | async-start | bytes 16515072 | tf_op jit(solution)/shard_map/all_gather | solution.py:141
  10.9 30.3 %copy-start.36 = (s32[512]{0:T(512)S(1)}, s32[512]{0:T(512)}, u32[]{:S(2)}) copy-start(s32[512]{0:T(512)} %param.22) | copy-start | bytes 6148
  10.9 356.3 %all-gather.5.cloned.1.call-start = ((), (), s32[]{:S(2)}) async-start(), calls=%async_computation.4 | async-start | bytes 11796480 | tf_op jit(solution)/shard_map/all_gather | solution.py:142
  12.2 203.5 %copy-start.2 = (bf16[512,1024]{1,0:T(8,128)(2,1)S(1)}, bf16[512,1024]{1,0:T(8,128)(2,1)}, u32[]{:S(2)}) copy-start(bf16[512,1024]{1,0:T(8,128)(2,1)} %param.20) | copy-start | bytes 3145732
  12.3 535.0 %reduce-scatter.8.cloned.1.call-start = ((), (), s32[]{:S(2)}) async-start(), calls=%async_computation.6 | async-start | bytes 11796480 | tf_op jit(solution)/shard_map/reduce_scatter | solution.py:261
  41.1 224.8 %copy-start.34 = (f32[1,8,4,128]{3,1,2,0:T(8,128)}, f32[1,8,4,128]{3,1,2,0:T(8,128)S(1)}, u32[]{:S(2)}) copy-start(f32[1,8,4,128]{3,1,2,0:T(8,128)S(1)} %copy.69) | copy-start | bytes 49156
  41.5 198.9 %copy-start.26 = (f32[512,16]{0,1:T(8,128)}, f32[512,16]{0,1:T(8,128)S(1)}, u32[]{:S(2)}) copy-start(f32[512,16]{0,1:T(8,128)S(1)} %get-tuple-element.106) | copy-start | bytes 98308
  41.5 198.9 %copy-start.28 = (f32[512,16]{0,1:T(8,128)}, f32[512,16]{0,1:T(8,128)S(1)}, u32[]{:S(2)}) copy-start(f32[512,16]{0,1:T(8,128)S(1)} %get-tuple-element.105) | copy-start | bytes 98308
  44.7 322.5 %copy-start.39 = (f32[512]{0:T(512)}, f32[512]{0:T(512)S(1)}, u32[]{:S(2)}) copy-start(f32[512]{0:T(512)S(1)} %compare_convert_fusion) | copy-start | bytes 6148
  44.7 221.2 %copy-start.41 = (f32[512]{0:T(512)}, f32[512]{0:T(512)S(1)}, u32[]{:S(2)}) copy-start(f32[512]{0:T(512)S(1)} %add_rsqrt_fusion) | copy-start | bytes 6148
  45.3 176.2 %copy-start.48 = (f32[1,1024]{1,0:T(1,128)}, f32[1,1024]{1,0:T(1,128)S(1)}, u32[]{:S(2)}) copy-start(f32[1,1024]{1,0:T(1,128)S(1)} %get-tuple-element.102) | copy-start | bytes 12292
  45.3 220.6 %copy-start.46 = (f32[1,1024]{1,0:T(1,128)}, f32[1,1024]{1,0:T(1,128)S(1)}, u32[]{:S(2)}) copy-start(f32[1,1024]{1,0:T(1,128)S(1)} %get-tuple-element.104) | copy-start | bytes 12292
  266.0 12.7 %copy-start.21 = (bf16[512,1024]{1,0:T(8,128)(2,1)S(1)}, bf16[512,1024]{1,0:T(8,128)(2,1)}, u32[]{:S(2)}) copy-start(bf16[512,1024]{1,0:T(8,128)(2,1)} %param.21) | copy-start | bytes 3145732
  287.6 498.9 %reduce-scatter.6.cloned.1.call-start = ((), (), s32[]{:S(2)}) async-start(), calls=%async_computation.5 | async-start | bytes 16515072 | tf_op jit(solution)/shard_map/reduce_scatter | solution.py:258
  381.1 14.5 %slice-start = ((s8[16777216]{0:T(1024)(128)(4,1)}), s8[4194304]{0:T(1024)(128)(4,1)S(1)}, s32[]{:S(2)}) async-start(s8[16777216]{0:T(1024)(128)(4,1)} %bitcast.38), calls=%async_computation.9 | async-start | bytes 8388608
  381.1 14.5 %slice-start.1 = ((s8[16777216]{0:T(1024)(128)(4,1)}), s8[4194304]{0:T(1024)(128)(4,1)S(1)}, s32[]{:S(2)}) async-start(s8[16777216]{0:T(1024)(128)(4,1)} %bitcast.38), calls=%async_computation.10 | async-start | bytes 8388608
  381.1 15.7 %slice-start.2 = ((s8[16777216]{0:T(1024)(128)(4,1)}), s8[4194304]{0:T(1024)(128)(4,1)S(1)}, s32[]{:S(2)}) async-start(s8[16777216]{0:T(1024)(128)(4,1)} %bitcast.38), calls=%async_computation.11 | async-start | bytes 8388608
  381.1 16.9 %slice-start.3 = ((s8[16777216]{0:T(1024)(128)(4,1)}), s8[4194304]{0:T(1024)(128)(4,1)S(1)}, s32[]{:S(2)}) async-start(s8[16777216]{0:T(1024)(128)(4,1)} %bitcast.38), calls=%async_computation.12 | async-start | bytes 8388608
  398.0 10.8 %copy-start.14 = (bf16[512,16,48]{0,2,1:T(8,128)(2,1)S(1)}, bf16[512,16,48]{0,2,1:T(8,128)(2,1)}, u32[]{:S(2)}) copy-start(bf16[512,16,48]{0,2,1:T(8,128)(2,1)} %copy-done.13) | copy-start | bytes 2359300
  398.0 10.8 %copy-start.25 = (bf16[512,16,16]{0,2,1:T(8,128)(2,1)S(1)}, bf16[512,16,16]{0,2,1:T(8,128)(2,1)}, u32[]{:S(2)}) copy-start(bf16[512,16,16]{0,2,1:T(8,128)(2,1)} %copy-done.24) | copy-start | bytes 786436
  458.1 393.3 %reduce-scatter.10.cloned.1.call-start = ((), (), s32[]{:S(2)}) async-start(), calls=%async_computation.7 | async-start | bytes 294912
  467.2 10.5 %copy-start.40 = (f32[512]{0:T(512)S(1)}, f32[512]{0:T(512)}, u32[]{:S(2)}) copy-start(f32[512]{0:T(512)} %copy-done.39) | copy-start | bytes 6148
  482.0 304.5 %copy-start.23 = (bf16[512,1024]{1,0:T(8,128)(2,1)S(1)}, bf16[512,1024]{1,0:T(8,128)(2,1)}, u32[]{:S(2)}) copy-start(bf16[512,1024]{1,0:T(8,128)(2,1)} %copy-done.22) | copy-start | bytes 3145732
  482.0 304.5 %copy-start.45 = (f32[1,1024]{1,0:T(1,128)S(1)}, f32[1,1024]{1,0:T(1,128)}, u32[]{:S(2)}) copy-start(f32[1,1024]{1,0:T(1,128)} %get-tuple-element.100) | copy-start | bytes 12292
  483.1 438.2 %all-reduce.3.cloned.1.call-start = ((), (), s32[]{:S(2)}) async-start(), calls=%async_computation.8 | async-start | bytes 6291456 | tf_op jit(solution)/shard_map/psum | solution.py:269
  786.5 71.4 %copy-start.38 = (f32[12,128]{1,0:T(8,128)S(1)}, f32[12,128]{1,0:T(8,128)}, u32[]{:S(2)}) copy-start(f32[12,128]{1,0:T(8,128)} %param.25) | copy-start | bytes 18436
  786.5 71.4 %copy-start.43 = (f32[12,128]{1,0:T(8,128)S(1)}, f32[12,128]{1,0:T(8,128)}, u32[]{:S(2)}) copy-start(f32[12,128]{1,0:T(8,128)} %param.28) | copy-start | bytes 18436
  786.5 71.4 %copy-start.44 = (f32[12,128]{1,0:T(8,128)S(1)}, f32[12,128]{1,0:T(8,128)}, u32[]{:S(2)}) copy-start(f32[12,128]{1,0:T(8,128)} %param.31) | copy-start | bytes 18436
  921.3 10.9 %copy-start.1 = (f32[640,1024]{1,0:T(8,128)S(1)}, f32[640,1024]{1,0:T(8,128)}, u32[]{:S(2)}) copy-start(f32[640,1024]{1,0:T(8,128)} %param.24) | copy-start | bytes 7864324
  921.3 10.9 %copy-start.15 = (f32[640,1024]{1,0:T(8,128)S(1)}, f32[640,1024]{1,0:T(8,128)}, u32[]{:S(2)}) copy-start(f32[640,1024]{1,0:T(8,128)} %param.27) | copy-start | bytes 7864324
  921.3 12.1 %copy-start.16 = (f32[640,1024]{1,0:T(8,128)S(1)}, f32[640,1024]{1,0:T(8,128)}, u32[]{:S(2)}) copy-start(f32[640,1024]{1,0:T(8,128)} %param.30) | copy-start | bytes 7864324
  921.3 12.4 %copy-start.18 = (bf16[640,1024]{1,0:T(8,128)(2,1)S(1)}, bf16[640,1024]{1,0:T(8,128)(2,1)}, u32[]{:S(2)}) copy-start(bf16[640,1024]{1,0:T(8,128)(2,1)} %get-tuple-element.67) | copy-start | bytes 3932164
  (28 other events, 171.9 us)
Sparse Core Ops, SparseCore 0:
  11.0 204.6 all-gather.2
  218.5 148.6 all-gather.4
  370.8 176.3 reduce-scatter.7
  550.7 235.7 reduce-scatter.5
  790.2 61.1 reduce-scatter.9
  853.8 67.4 all-reduce.2
where the time goes:
time: 956 us; the launch traced here: 945 us
  waiting for transfers between devices  670 us (70%)
  matrix products  119 us (12%)
  other arithmetic  74.3 us (8%)
  blocking collectives  34.4 us (4%)
  local copies, waits for them, and re-layouts  32.3 us (3%)
  between operations  15.2 us (2%)
    reduce_scatter x1, waiting for transfers between devices, shards(): lax.psum_scatter(grad_in_term.astype(jnp.bfloat16), 'shard', scatter_dime...  239 us
    all_gather x1, waiting for transfers between devices, shards(): lax.all_gather(master_in.astype(jnp.bfloat16), 'shard', axis=0, tiled=True)  170 us
    all_gather x1, waiting for transfers between devices, shards(): lax.all_gather(master_out.astype(jnp.bfloat16), 'shard', axis=0, tiled=True)  79.6 us
    reduce_scatter x1, waiting for transfers between devices, shards(): lax.psum_scatter(grad_out_term.astype(jnp.bfloat16), 'shard', scatter_dim...  64.1 us
    psum x1, waiting for transfers between devices, shards(): lax.psum(part_in.astype(jnp.bfloat16), 'grp').astype(jnp.float32)  62.7 us
    unnamed x7, waiting for transfers between devices  53.8 us
    all_gather x1, blocking collectives, shards(): lax.all_gather(vectors.astype(jnp.bfloat16), 'shard', axis=1, tiled=True)  28.7 us
    dot_general x3, matrix products, contract_cols(): lax.dot_general(left, right, (((1,), (1,)), ((), ())), preferred_element_...  26.9 us
  transfers between devices with their start and end apart: 6, of which 6 were waited for; matrix products, arithmetic and copies ran while one was open for 20% of the time, Pallas kernels for 0%

commit v1 on v0

--- a/solution.py
+++ b/solution.py
@@ -266,7 +266,7 @@
         ).astype(jnp.float32),
     )
     grad_in, grad_out, grad_vec = (
-        lax.psum(part_in.astype(jnp.bfloat16), "grp").astype(jnp.float32),
+        jnp.sum(lax.all_gather(part_in.astype(jnp.bfloat16), "grp"), axis=0).astype(jnp.float32),
         lax.psum(part_out.astype(jnp.bfloat16), "grp").astype(jnp.float32),
         lax.psum(part_vec.astype(jnp.bfloat16), "grp").astype(jnp.float32),
     )

time: 956 us -> 1130 us (1.18)
  waiting for transfers between devices: 670 us -> 851 us
    reduce_scatter x1, waiting for transfers between devices: 64.1 us -> 176 us  [shards(): lax.psum_scatter(grad_out_term.astype(jnp.bfloat16), 'shard', scatter_dim...]
    all_gather x1, waiting for transfers between devices: 79.6 us -> 151 us  [shards(): lax.all_gather(master_out.astype(jnp.bfloat16), 'shard', axis=0, tiled=True)]
    all_gather x0 -> x1, waiting for transfers between devices: none -> 45.6 us  [shards(): lax.all_gather(part_in.astype(jnp.bfloat16), 'grp')]
    reduce_scatter x1, waiting for transfers between devices: 239 us -> 210 us  [shards(): lax.psum_scatter(grad_in_term.astype(jnp.bfloat16), 'shard', scatter_dime...]
    psum x1, waiting for transfers between devices: 62.7 us -> 40.6 us  [shards(): lax.psum(part_out.astype(jnp.bfloat16), 'grp').astype(jnp.float32)]
    unnamed x7 -> x8, waiting for transfers between devices: 53.8 us -> 53.8 us
  transfers between devices with their start and end apart: 6 -> 7, of which waited for: 6 -> 7; matrix products, arithmetic and copies ran while one was open for 20% -> 4% of each run, Pallas kernels for 0% -> 0%
where the time goes in v1:
time: 1130 us; the launch traced here: 1120 us
  waiting for transfers between devices  851 us (75%)
  matrix products  126 us (11%)
  other arithmetic  73.4 us (6%)
  blocking collectives  34.6 us (3%)
  local copies, waits for them, and re-layouts  24.3 us (2%)
  between operations  15.2 us (1%)
    reduce_scatter x1, waiting for transfers between devices, shards(): lax.psum_scatter(grad_in_term.astype(jnp.bfloat16), 'shard', scatter_dime...  210 us
    reduce_scatter x1, waiting for transfers between devices, shards(): lax.psum_scatter(grad_out_term.astype(jnp.bfloat16), 'shard', scatter_dim...  176 us
    all_gather x1, waiting for transfers between devices, shards(): lax.all_gather(master_in.astype(jnp.bfloat16), 'shard', axis=0, tiled=True)  173 us
    all_gather x1, waiting for transfers between devices, shards(): lax.all_gather(master_out.astype(jnp.bfloat16), 'shard', axis=0, tiled=True)  151 us
    unnamed x8, waiting for transfers between devices  53.8 us
    all_gather x1, waiting for transfers between devices, shards(): lax.all_gather(part_in.astype(jnp.bfloat16), 'grp')  45.6 us
    psum x1, waiting for transfers between devices, shards(): lax.psum(part_out.astype(jnp.bfloat16), 'grp').astype(jnp.float32)  40.6 us
    all_gather x1, blocking collectives, shards(): lax.all_gather(vectors.astype(jnp.bfloat16), 'shard', axis=1, tiled=True)  28.7 us
  transfers between devices with their start and end apart: 7, of which 7 were waited for; matrix products, arithmetic and copies ran while one was open for 4% of the time, Pallas kernels for 0%

profile of v1, /device:TPU:0, one launch (start us, length us, event | category | flops | bytes accessed | tf_op | source)
XLA Modules:
  0.0 1124.4 jit_solution(14135593474857481716)
XLA Ops:
  10.9 28.7 %all_gather.15 = bf16[12,1024]{1,0:T(8,128)(2,1)S(1)} all-gather(bf16[12,128]{1,0:T(8,128)(2,1)S(1)} %convert_element_type.107), channel_id=1, replica_groups=mesh['grp'=4,'shard'=8] {'shard'}, dimensions={1}, use_global_device_ids=true | all-gather | bytes 27648 | tf_op jit(solution)/shard_map/all_gather | solution.py:143
  42.3 173.3 %all-gather.5.cloned.1.call-done = bf16[1024,7168]{1,0:T(8,128)(2,1)} async-done(((bf16[128,7168]{1,0:T(8,128)(2,1)}), bf16[1024,7168]{1,0:T(8,128)(2,1)}) %all-gather.5.cloned.1.call-update) | async-done | bytes 14680080 | tf_op jit(solution)/shard_map/all_gather | solution.py:141
  215.6 5.8 fusion.20
  238.6 10.0 fusion.91
  248.6 8.3 fusion
  256.9 7.5 fusion.55
  265.0 10.5 multiply_convert_fusion.1
  277.6 8.8 convolution_convert_fusion
  286.5 176.5 %reduce-scatter.8.cloned.1.call-done = bf16[640,1024]{1,0:T(8,128)(2,1)} async-done(((bf16[5120,1024]{1,0:T(8,128)(2,1)}), bf16[640,1024]{1,0:T(8,128)(2,1)}) %reduce-scatter.8.cloned.1.call-update) | async-done | bytes 1310736 | tf_op jit(solution)/shard_map/reduce_scatter | solution.py:261
  463.1 40.6 %all-reduce.2.cloned.1.call-done = bf16[640,1024]{1,0:T(8,128)(2,1)} async-done(((bf16[640,1024]{1,0:T(8,128)(2,1)}), bf16[640,1024]{1,0:T(8,128)(2,1)}) %all-reduce.2.cloned.1.call-update) | async-done | bytes 1310736 | tf_op jit(solution)/shard_map/psum | solution.py:270
  503.7 8.2 add_multiply_fusion.1
  512.0 150.6 %all-gather.7.cloned.1.call-done = bf16[5120,1024]{1,0:T(8,128)(2,1)} async-done(((bf16[640,1024]{1,0:T(8,128)(2,1)}), bf16[5120,1024]{1,0:T(8,128)(2,1)}) %all-gather.7.cloned.1.call-update) | async-done | bytes 10485776 | tf_op jit(solution)/shard_map/all_gather | solution.py:142
  662.6 8.9 fusion.67
  671.5 3.8 copy-done.3
  676.1 9.6 fusion.56
  685.7 13.9 %multiply_reduce_fusion = (f32[16,512]{1,0:T(8,128)}, f32[16,512,512]{1,2,0:T(8,128)}) fusion(f32[16,512,512]{1,2,0:T(8,128)} %get-tuple-element.109, f32[16,512]{1,0:T(8,128)} %copy-done.19, bf16[512,16,64]{0,2,1:T(8,128)(2,1)S(1)} %bitcast.42, bf16[512,16,64]{0,2,1:T(8,128)(2,1)} %bitcast.56), kind=kOutput, calls=%fused_computation.1 | convolution fusion | flops 549445632 | bytes 35717120 | tf_op jit(solution)/shard_map/qhd,khd->hqk/dot_general | solution.py:205
  699.7 10.6 multiply_convert_fusion
  710.3 6.5 multiply_bitcast_fusion
  720.3 6.5 fusion.85
  726.9 5.7 convolution_convert_fusion.1
  733.9 6.9 convolution_convert_fusion.2
  740.8 10.5 pad_maximum_fusion
  751.4 8.5 fusion.12
  760.0 9.4 fusion.48
  770.5 4.4 fusion.53
  776.1 210.3 %reduce-scatter.6.cloned.1.call-done = bf16[128,7168]{1,0:T(8,128)(2,1)} async-done(((bf16[1024,7168]{1,0:T(8,128)(2,1)}), bf16[128,7168]{1,0:T(8,128)(2,1)}) %reduce-scatter.6.cloned.1.call-update) | async-done | bytes 1835024 | tf_op jit(solution)/shard_map/reduce_scatter | solution.py:258
  986.5 11.3 %fusion.52 = bf16[512,1024]{1,0:T(8,128)(2,1)} fusion(bf16[512,1024]{1,0:T(8,128)(2,1)S(1)} %copy-done.2, bf16[5120,1024]{1,0:T(8,128)(2,1)} %all-gather.7.cloned.1.call-done, bf16[512,4096]{1,0:T(8,128)(2,1)} %copy-done.40, bf16[512,1024]{1,0:T(8,128)(2,1)S(1)} %copy-done.17, f32[512]{0:T(512)S(1)} %copy-done.30, f32[1024]{0:T(1024)S(1)} %bitcast.76), kind=kOutput, calls=%fused_computation.73 | convolution fusion | flops 5381816320 | bytes 17831936 | tf_op jit(solution)/shard_map/dot_general | solution.py:189
  997.7 53.7 %reduce-scatter.10.cloned.1.call-done = bf16[128,12]{1,0:T(8,128)(2,1)} async-done(((bf16[1024,12]{1,0:T(8,128)(2,1)}), bf16[128,12]{1,0:T(8,128)(2,1)}) %reduce-scatter.10.cloned.1.call-update) | async-done | bytes 3088
  1052.2 5.9 psum.15
  1058.7 45.6 %all-gather.9.cloned.1.call-done = bf16[512,7168]{1,0:T(8,128)(2,1)} async-done(((bf16[128,7168]{1,0:T(8,128)(2,1)}), bf16[512,7168]{1,0:T(8,128)(2,1)}) %all-gather.9.cloned.1.call-update) | async-done | bytes 7340048 | tf_op jit(solution)/shard_map/all_gather | solution.py:269
  1104.3 4.6 reduce_sum.173
  1108.9 8.4 add_multiply_fusion
  (168 shorter events, 35.5 us)
Async XLA Ops:
  7.2 32.5 %copy-start.26 = (s32[512]{0:T(512)S(1)}, s32[512]{0:T(512)}, u32[]{:S(2)}) copy-start(s32[512]{0:T(512)} %param.22) | copy-start | bytes 6148
  7.2 32.9 %copy-start.1 = (bf16[512,1024]{1,0:T(8,128)(2,1)S(1)}, bf16[512,1024]{1,0:T(8,128)(2,1)}, u32[]{:S(2)}) copy-start(bf16[512,1024]{1,0:T(8,128)(2,1)} %param.20) | copy-start | bytes 3145732
  7.2 208.4 %all-gather.5.cloned.1.call-start = ((), (), s32[]{:S(2)}) async-start(), calls=%async_computation.3 | async-start | bytes 16515072 | tf_op jit(solution)/shard_map/all_gather | solution.py:141
  10.9 452.1 %reduce-scatter.8.cloned.1.call-start = ((), (), s32[]{:S(2)}) async-start(), calls=%async_computation.6 | async-start | bytes 11796480 | tf_op jit(solution)/shard_map/reduce_scatter | solution.py:261
  39.7 225.3 %copy-start.24 = (f32[1,8,4,128]{3,1,2,0:T(8,128)}, f32[1,8,4,128]{3,1,2,0:T(8,128)S(1)}, u32[]{:S(2)}) copy-start(f32[1,8,4,128]{3,1,2,0:T(8,128)S(1)} %copy.69) | copy-start | bytes 49156
  40.1 196.4 %copy-start.20 = (f32[512,16]{0,1:T(8,128)}, f32[512,16]{0,1:T(8,128)S(1)}, u32[]{:S(2)}) copy-start(f32[512,16]{0,1:T(8,128)S(1)} %get-tuple-element.105) | copy-start | bytes 98308
  40.1 196.4 %copy-start.22 = (f32[512,16]{0,1:T(8,128)}, f32[512,16]{0,1:T(8,128)S(1)}, u32[]{:S(2)}) copy-start(f32[512,16]{0,1:T(8,128)S(1)} %get-tuple-element.104) | copy-start | bytes 98308
  40.8 621.8 %copy-start.29 = (f32[512]{0:T(512)}, f32[512]{0:T(512)S(1)}, u32[]{:S(2)}) copy-start(f32[512]{0:T(512)S(1)} %compare_convert_fusion) | copy-start | bytes 6148
  40.8 224.2 %copy-start.31 = (f32[512]{0:T(512)}, f32[512]{0:T(512)S(1)}, u32[]{:S(2)}) copy-start(f32[512]{0:T(512)S(1)} %add_rsqrt_fusion) | copy-start | bytes 6148
  41.4 180.0 %copy-start.36 = (f32[1,1024]{1,0:T(1,128)}, f32[1,1024]{1,0:T(1,128)S(1)}, u32[]{:S(2)}) copy-start(f32[1,1024]{1,0:T(1,128)S(1)} %get-tuple-element.101) | copy-start | bytes 12292
  41.4 223.6 %copy-start.38 = (f32[1,1024]{1,0:T(1,128)}, f32[1,1024]{1,0:T(1,128)S(1)}, u32[]{:S(2)}) copy-start(f32[1,1024]{1,0:T(1,128)S(1)} %get-tuple-element.103) | copy-start | bytes 12292
  236.5 20.4 %copy-start.6 = (bf16[512,1024]{0,1:T(8,128)(2,1)}, bf16[512,1024]{0,1:T(8,128)(2,1)S(1)}, u32[]{:S(2)}) copy-start(bf16[512,1024]{0,1:T(8,128)(2,1)S(1)} %copy.52) | copy-start | bytes 3145732
  265.0 10.5 copy-start.16
  265.0 12.6 %copy-start.15 = (bf16[512,1024]{1,0:T(8,128)(2,1)S(1)}, bf16[512,1024]{1,0:T(8,128)(2,1)}, u32[]{:S(2)}) copy-start(bf16[512,1024]{1,0:T(8,128)(2,1)} %param.21) | copy-start | bytes 3145732
  286.4 217.2 %copy-start.11 = (f32[640,1024]{1,0:T(8,128)S(1)}, f32[640,1024]{1,0:T(8,128)}, u32[]{:S(2)}) copy-start(f32[640,1024]{1,0:T(8,128)} %param.24) | copy-start | bytes 7864324
  286.5 217.2 %all-reduce.2.cloned.1.call-start = ((), (), s32[]{:S(2)}) async-start(), calls=%async_computation.7 | async-start | bytes 2621440 | tf_op jit(solution)/shard_map/psum | solution.py:270
  463.0 199.5 %all-gather.7.cloned.1.call-start = ((), (), s32[]{:S(2)}) async-start(), calls=%async_computation.4 | async-start | bytes 11796480 | tf_op jit(solution)/shard_map/all_gather | solution.py:142
  511.9 474.5 %reduce-scatter.6.cloned.1.call-start = ((), (), s32[]{:S(2)}) async-start(), calls=%async_computation.5 | async-start | bytes 16515072 | tf_op jit(solution)/shard_map/reduce_scatter | solution.py:258
  511.9 164.1 %copy-start.19 = (f32[16,512]{1,0:T(8,128)}, f32[16,512]{1,0:T(8,128)S(1)}, u32[]{:S(2)}) copy-start(f32[16,512]{1,0:T(8,128)S(1)} %log_add_fusion) | copy-start | bytes 98308
  676.1 23.5 %slice-start = ((s8[16777216]{0:T(1024)(128)(4,1)}), s8[4194304]{0:T(1024)(128)(4,1)S(1)}, s32[]{:S(2)}) async-start(s8[16777216]{0:T(1024)(128)(4,1)} %bitcast.39), calls=%async_computation.10 | async-start | bytes 8388608
  676.1 23.5 %slice-start.1 = ((s8[16777216]{0:T(1024)(128)(4,1)}), s8[4194304]{0:T(1024)(128)(4,1)S(1)}, s32[]{:S(2)}) async-start(s8[16777216]{0:T(1024)(128)(4,1)} %bitcast.39), calls=%async_computation.11 | async-start | bytes 8388608
  685.7 13.9 %slice-start.2 = ((s8[16777216]{0:T(1024)(128)(4,1)}), s8[4194304]{0:T(1024)(128)(4,1)S(1)}, s32[]{:S(2)}) async-start(s8[16777216]{0:T(1024)(128)(4,1)} %bitcast.39), calls=%async_computation.12 | async-start | bytes 8388608
  685.7 13.9 %slice-start.3 = ((s8[16777216]{0:T(1024)(128)(4,1)}), s8[4194304]{0:T(1024)(128)(4,1)S(1)}, s32[]{:S(2)}) async-start(s8[16777216]{0:T(1024)(128)(4,1)} %bitcast.39), calls=%async_computation.13 | async-start | bytes 8388608
  699.6 17.1 %copy-start.14 = (bf16[512,16,16]{0,2,1:T(8,128)(2,1)S(1)}, bf16[512,16,16]{0,2,1:T(8,128)(2,1)}, u32[]{:S(2)}) copy-start(bf16[512,16,16]{0,2,1:T(8,128)(2,1)} %copy-done.13) | copy-start | bytes 786436
  751.4 300.0 %reduce-scatter.10.cloned.1.call-start = ((), (), s32[]{:S(2)}) async-start(), calls=%async_computation.9 | async-start | bytes 294912
  760.0 10.5 copy-start.30
  770.5 215.9 %copy-start.17 = (bf16[512,1024]{1,0:T(8,128)(2,1)S(1)}, bf16[512,1024]{1,0:T(8,128)(2,1)}, u32[]{:S(2)}) copy-start(bf16[512,1024]{1,0:T(8,128)(2,1)} %copy-done.16) | copy-start | bytes 3145732
  770.5 215.9 %copy-start.35 = (f32[1,1024]{1,0:T(1,128)S(1)}, f32[1,1024]{1,0:T(1,128)}, u32[]{:S(2)}) copy-start(f32[1,1024]{1,0:T(1,128)} %get-tuple-element.99) | copy-start | bytes 12292
  776.0 328.3 %all-gather.9.cloned.1.call-start = ((), (), s32[]{:S(2)}) async-start(), calls=%async_computation.8 | async-start | bytes 9175040 | tf_op jit(solution)/shard_map/all_gather | solution.py:269
  986.4 71.6 %copy-start.28 = (f32[12,128]{1,0:T(8,128)S(1)}, f32[12,128]{1,0:T(8,128)}, u32[]{:S(2)}) copy-start(f32[12,128]{1,0:T(8,128)} %param.25) | copy-start | bytes 18436
  986.4 71.6 %copy-start.33 = (f32[12,128]{1,0:T(8,128)S(1)}, f32[12,128]{1,0:T(8,128)}, u32[]{:S(2)}) copy-start(f32[12,128]{1,0:T(8,128)} %param.28) | copy-start | bytes 18436
  986.5 71.6 %copy-start.34 = (f32[12,128]{1,0:T(8,128)S(1)}, f32[12,128]{1,0:T(8,128)}, u32[]{:S(2)}) copy-start(f32[12,128]{1,0:T(8,128)} %param.31) | copy-start | bytes 18436
  (23 other events, 128.6 us)
Sparse Core Ops, SparseCore 0:
  11.0 204.5 all-gather.4
  286.6 176.3 reduce-scatter.7
  465.4 38.2 all-reduce.1
  512.0 150.5 all-gather.6
  751.5 234.8 reduce-scatter.5
  990.1 61.1 reduce-scatter.9
  1052.9 51.3 all-gather.8
